TPU v7x, 32 devices: a whole 2x2x4 slice. The times are simulated.
32 devices in a mesh: dp: 4 (over z), ctx: 4 (over y, core), tp: 2 (over x).
Axes of the slice: x: 2, y: 2, z: 4, core: 2. Of those that a mesh axis runs over, the one named last changes fastest.
Arguments:
- queries: bfloat16 [4, 512, 4096], P('dp', 'ctx', 'tp'), may hold values from -8 to 8
- keys_text: bfloat16 [4, 512, 512], P('dp', 'ctx', 'tp'), may hold values from -8 to 8
- values_text: bfloat16 [4, 512, 512], P('dp', 'ctx', 'tp'), may hold values from -6 to 6
- patch_rows: bfloat16 [4, 4, 8, 2, 512], P('dp', 'ctx', None, None, 'tp'), may hold values from -6 to 6
- patch_owner: int32 [4, 4, 8, 1], P('dp', 'ctx'), may hold values from 0 to 3; in each aligned block of 8 rows (0 to 7, 8 to 15, ..., all dimensions but the last counted through in order) at most 4 rows name the same one
- patch_place: int32 [4, 4, 8], P('dp', 'ctx'), may hold values from 0 to 127
- value_head: bfloat16 [4096], P('tp'), may hold values from -0.75 to 0.75
Outputs:
- attention: bfloat16 [4, 512, 4096], P('dp', 'ctx', 'tp')
- value_out: float32 [4, 512], P('dp', 'ctx')
Inputs may be any that keep to these rules, and one draw needn't show every extreme that they name: `patch_owner`: among the rows of one vision shard at most 4 name the same sequence, and exactly 4 do in some shards. `patch_place`: rows that share an owner, a ctx index and a position are all added there.
All inputs are finite; a program needn't handle non-finite values.
Results may differ from a plain program's by a relative error of at most 0.0079.
Values may be sent and summed in bfloat16 or wider, within the bound.
A program may use at most 64 MiB of HBM per device.

v0:
```python
import jax
import jax.numpy as jnp
from jax import lax
from jax.sharding import PartitionSpec as P

HD = 128
CAP = 4


def attend_block(
    carried, query_split, query_place, block_keys, block_values, key_place, score_scale
):
    running_max, denominator, numerator = carried
    scores = (
        jnp.einsum("tgrd,sgd->tgrs", query_split, block_keys, preferred_element_type=jnp.float32)
        * score_scale
    )
    allowed = (key_place[None, :] <= query_place[:, None])[:, None, None, :]
    scores = jnp.where(allowed, scores, -1e30)
    new_max = jnp.maximum(running_max, jnp.max(scores, axis=-1))
    weights = jnp.where(allowed, jnp.exp(scores - new_max[..., None]), 0.0)
    shrink = jnp.exp(running_max - new_max)
    denominator = denominator * shrink + jnp.sum(weights, axis=-1)
    numerator = numerator * shrink[..., None] + jnp.einsum(
        "tgrs,sgd->tgrd",
        weights.astype(jnp.bfloat16),
        block_values,
        preferred_element_type=jnp.float32,
    )
    return (new_max, denominator, numerator)


def unchanged(carried):
    return carried


def body(queries, keys_text, values_text, patch_rows, patch_owner, patch_place, value_head):
    token_count = queries.shape[1]
    kv_width = keys_text.shape[2]
    groups = kv_width // HD
    head_count = queries.shape[2] // HD
    group_size = head_count // groups
    score_scale = HD ** (-0.5)
    dp_count = lax.axis_size("dp")
    slot_count = dp_count * CAP
    owner_seq = patch_owner[0, 0, :, 0]
    places = patch_place[0, 0]
    owner_hits = (owner_seq[:, None] == jnp.arange(dp_count, dtype=jnp.int32)[None, :]).astype(
        jnp.int32
    )
    before = jnp.cumsum(owner_hits, axis=0) - owner_hits
    slot_rank = jnp.sum(before * owner_hits, axis=1)
    target = owner_seq * CAP + slot_rank
    select = (jnp.arange(slot_count, dtype=jnp.int32)[:, None] == target[None, :]).astype(jnp.int32)
    row_data = patch_rows[0, 0].reshape(places.shape[0], 2 * kv_width)
    packed = jnp.dot(
        select.astype(jnp.bfloat16), row_data, preferred_element_type=jnp.float32
    ).astype(jnp.bfloat16)
    filled = jnp.sum(select, axis=1)
    slot_place = jnp.sum(select * places[None, :], axis=1) + (1 - filled) * token_count
    packed = packed.reshape(slot_count, 2, kv_width)
    arrived, arrived_place = (
        lax.all_to_all(packed, "dp", split_axis=0, concat_axis=0, tiled=True),
        lax.all_to_all(slot_place, "dp", split_axis=0, concat_axis=0, tiled=True),
    )
    landing = (jnp.arange(token_count, dtype=jnp.int32)[:, None] == arrived_place[None, :]).astype(
        jnp.bfloat16
    )
    arrivals = jnp.dot(
        landing, arrived.reshape(slot_count, 2 * kv_width), preferred_element_type=jnp.float32
    )
    merged_keys = (keys_text[0].astype(jnp.float32) + arrivals[:, :kv_width]).astype(jnp.bfloat16)
    merged_values = (values_text[0].astype(jnp.float32) + arrivals[:, kv_width:]).astype(
        jnp.bfloat16
    )
    query_split = queries[0].reshape(token_count, groups, group_size, HD)
    first_row = lax.axis_index("ctx") * token_count
    query_place = first_row + jnp.arange(token_count, dtype=jnp.int32)
    initial = (
        jnp.full((token_count, groups, group_size), -1e30, jnp.float32),
        jnp.zeros((token_count, groups, group_size), jnp.float32),
        jnp.zeros((token_count, groups, group_size, HD), jnp.float32),
    )
    carried = initial
    start_row = jnp.int32(0)
    piece_keys = lax.all_gather(merged_keys, "ctx", axis=0, tiled=True)
    piece_values = lax.all_gather(merged_values, "ctx", axis=0, tiled=True)
    piece_rows = piece_keys.shape[0]
    block_rows = min(512, piece_rows)
    for lower in range(0, piece_rows, block_rows):
        upper = min(lower + block_rows, piece_rows)
        block_keys = piece_keys[lower:upper].reshape(upper - lower, groups, HD)
        block_values = piece_values[lower:upper].reshape(upper - lower, groups, HD)
        key_place = start_row + lower + jnp.arange(upper - lower, dtype=jnp.int32)

        def update(state_in):
            return attend_block(
                state_in, query_split, query_place, block_keys, block_values, key_place, score_scale
            )

        carried = lax.cond(
            start_row + lower <= first_row + token_count - 1, update, unchanged, carried
        )
    running_max, denominator, numerator = carried
    attention = (
        (numerator / denominator[..., None])
        .reshape(token_count, head_count * HD)
        .astype(jnp.bfloat16)
    )
    partial_value = jnp.dot(attention, value_head, preferred_element_type=jnp.float32)
    value_out = lax.psum(partial_value, "tp")
    return (attention[None], value_out[None])


def solution(mesh):
    in_specs = (
        P("dp", "ctx", "tp"),
        P("dp", "ctx", "tp"),
        P("dp", "ctx", "tp"),
        P("dp", "ctx", None, None, "tp"),
        P("dp", "ctx", None, None),
        P("dp", "ctx", None),
        P("tp"),
    )
    out_specs = (P("dp", "ctx", "tp"), P("dp", "ctx"))
    return jax.shard_map(body, mesh=mesh, in_specs=in_specs, out_specs=out_specs, check_vma=False)
```

profile of v0, /device:TPU:0, one launch (start us, length us, event | category | flops | bytes accessed | tf_op | source)
XLA Modules:
  0.0 53.5 jit_solution(15466480431015100622)
XLA Ops:
  0.6 0.7 %fusion.25 = s32[8,4]{0,1:T(4,128)S(1)} fusion(s32[8]{0:T(128)} %bitcast.58), kind=kLoop, calls=%fused_computation.37 | loop fusion | flops 64 | bytes 160 | tf_op jit(solution)/shard_map/convert_element_type | solution.py:48
  1.3 0.2 reduce_window_sum.11
  1.5 0.7 %select_reduce_fusion.1 = s32[8]{0:T(128)S(1)} fusion(s32[8,4]{0,1:T(4,128)S(1)} %reduce_window_sum.11, s32[8]{0:T(128)} %bitcast.59), kind=kLoop, calls=%fused_computation.35 | loop fusion | flops 152 | bytes 192 | tf_op jit(solution)/shard_map/reduce_sum | solution.py:52
  2.2 0.7 %multiply_add_fusion.1 = s32[8]{0:T(128)S(1)} fusion(s32[8]{0:T(128)S(1)} %select_reduce_fusion.1, s32[1,1,8,1]{2,3,1,0:T(1,128)} %param.13), kind=kLoop, calls=%fused_computation.39 | loop fusion | flops 16 | bytes 96 | tf_op jit(solution)/shard_map/add | solution.py:53
  2.8 0.7 %convert_reduce_fusion = (s32[16]{0:T(128)S(1)}, s32[16]{0:T(128)S(1)}) fusion(s32[8]{0:T(128)S(1)} %multiply_add_fusion.1, s32[8]{0:T(128)} %bitcast.60), kind=kLoop, calls=%fused_computation.31 | loop fusion | flops 608 | bytes 192 | tf_op jit(solution)/shard_map/reduce_sum | solution.py:59
  3.6 0.7 %add.48 = s32[4,4,1]{1,0,2:T(4,128)} reshape(s32[16]{0:T(128)S(1)} %multiply_add_fusion) | data formatting | bytes 128 | tf_op jit(solution)/shard_map/add | solution.py:60
  4.2 6.3 %all-to-all-start = ((s32[4,4,1]{1,2,0:T(1,128)}), s32[4,4,1]{1,2,0:T(1,128)S(1)}, u32[]{:S(2)}, u32[]{:S(2)}) async-start(s32[4,4,1]{1,2,0:T(1,128)} %bitcast.7), calls=%async_computation | async-start | bytes 4096 | tf_op jit(solution)/shard_map/all_to_all | solution.py:64
  10.6 0.7 %copy.45 = bf16[1,8,2,256]{3,1,2,0:T(8,128)(2,1)S(1)} copy(bf16[1,8,2,256]{3,2,1,0:T(2,128)(2,1)} %bitcast.56) | data formatting | bytes 16384
  11.3 0.3 convolution_convert_fusion
  11.5 0.6 %reshape.108 = bf16[16,2,256]{2,1,0:T(2,128)(2,1)} reshape(bf16[16,512]{1,0:T(8,128)(2,1)S(1)} %convolution_convert_fusion) | data formatting | bytes 32768 | tf_op jit(solution)/shard_map/reshape | solution.py:61
  12.2 3.8 %all-to-all-done = s32[4,4,1]{1,2,0:T(1,128)S(1)} async-done(((s32[4,4,1]{1,2,0:T(1,128)}), s32[4,4,1]{1,2,0:T(1,128)S(1)}, u32[]{:S(2)}, u32[]{:S(2)}) %all-to-all-start) | async-done | bytes 96 | tf_op jit(solution)/shard_map/all_to_all | solution.py:64
  16.0 3.3 %all-to-all-start.1 = ((bf16[16,2,256]{2,1,0:T(2,128)(2,1)}), bf16[16,2,256]{2,1,0:T(2,128)(2,1)S(1)}, u32[]{:S(2)}, u32[]{:S(2)}) async-start(bf16[16,2,256]{2,1,0:T(2,128)(2,1)} %reshape.108), calls=%async_computation.1 | async-start | bytes 32768 | tf_op jit(solution)/shard_map/all_to_all | solution.py:63
  19.3 0.7 %reshape.114 = bf16[2048,1]{0,1:T(2,128)(2,1)S(1)} reshape(bf16[2048]{0:T(1024)(128)(2,1)} %param.15) | data formatting | bytes 8192 | tf_op args[6]
  20.0 0.6 %broadcast.91 = s32[]{:T(128)} broadcast(s32[]{:T(128)} %constant.11.clone.1), dimensions={} | broadcast | bytes 8 | tf_op jit(solution)/shard_map/all_to_all | solution.py:64
  20.6 0.7 %reduce.3 = s32[4,4]{1,0:T(4,128)S(1)} reduce(s32[4,4,1]{1,2,0:T(1,128)S(1)} %all-to-all-done, s32[]{:T(128)} %broadcast.91), dimensions={2}, to_apply=%all_to_all.7.reduce_sub_computation.3 | reduce | bytes 132 | tf_op jit(solution)/shard_map/all_to_all | solution.py:64
  21.4 3.5 %all-to-all-done.1 = bf16[16,2,256]{2,1,0:T(2,128)(2,1)S(1)} async-done(((bf16[16,2,256]{2,1,0:T(2,128)(2,1)}), bf16[16,2,256]{2,1,0:T(2,128)(2,1)S(1)}, u32[]{:S(2)}, u32[]{:S(2)}) %all-to-all-start.1) | async-done | bytes 16416 | tf_op jit(solution)/shard_map/all_to_all | solution.py:63
  24.9 0.2 fusion.22
  25.0 0.9 %fusion.20 = (bf16[128,256]{1,0:T(8,128)(2,1)S(1)}, bf16[128,256]{1,0:T(8,128)(2,1)S(1)}) fusion(f32[128,512]{1,0:T(8,128)S(1)} %fusion.22, bf16[1,128,256]{2,1,0:T(8,128)(2,1)} %param.11, bf16[1,128,256]{2,1,0:T(8,128)(2,1)} %param.10), kind=kLoop, calls=%fused_computation.24 | loop fusion | flops 196608 | bytes 524288 | tf_op jit(solution)/shard_map/convert_element_type | solution.py:73
  25.9 5.8 %all_gather.6 = bf16[512,256]{1,0:T(8,128)(2,1)S(1)} all-gather(bf16[128,256]{1,0:T(8,128)(2,1)S(1)} %get-tuple-element.45), channel_id=1, replica_groups=mesh['dp'=4,'ctx'=4,'tp'=2] {'ctx'}, dimensions={0}, use_global_device_ids=true | all-gather | bytes 327680 | tf_op jit(solution)/shard_map/all_gather | solution.py:86
  31.7 5.8 %all_gather.7 = bf16[512,256]{1,0:T(8,128)(2,1)S(1)} all-gather(bf16[128,256]{1,0:T(8,128)(2,1)S(1)} %get-tuple-element.44), channel_id=1, replica_groups=mesh['dp'=4,'ctx'=4,'tp'=2] {'ctx'}, dimensions={0}, use_global_device_ids=true | all-gather | bytes 327680 | tf_op jit(solution)/shard_map/all_gather | solution.py:87
  37.6 9.2 %conditional.1 = (f32[128,2,8]{0,2,1:T(8,128)S(1)}, f32[128,2,8,128]{0,3,2,1:T(8,128)S(1)}) conditional(s32[]{:T(128)} %convert_element_type.53, () %tuple.16, (s32[512]{0:T(512)S(1)}, s32[]{:T(128)}, s32[128]{0:T(128)S(1)}, bf16[512,256]{1,0:T(8,128)(2,1)S(1)}, bf16[1,128,2048]{2,1,0:T(8,128)(2,1)}, /*index=5*/bf16[512,256]{1,0:T(8,128)(2,1)S(1)}) %tuple.17), branch_computations={%region_4.5_spmd, %region_5.8_spmd} | conditional | flops 550836352 | bytes 36007472 | solution.py:101
  37.6 0.1 broadcast_compare_fusion
  37.7 1.1 %copy.44 = bf16[16,8,16,128]{3,2,1,0:T(8,128)(2,1)S(1)} copy(bf16[16,8,16,128]{3,1,2,0:T(8,128)(2,1)} %bitcast.52) | data formatting | bytes 1048576 | tf_op jit(solution)/shard_map/cond
  38.9 0.8 %fusion = (f32[128,2,8]{0,2,1:T(8,128)S(1)}, f32[2,512,128,8]{2,1,3,0:T(8,128)S(1)}) fusion(pred[128,512]{0,1:T(8,128)(4,1)S(1)} %broadcast_compare_fusion, bf16[128,2,8,128]{3,2,1,0:T(8,128)(2,1)S(1)} %bitcast.50, bf16[512,2,128,1]{2,1,0,3:T(2,128)(2,1)S(1)} %bitcast.51), kind=kOutput, calls=%fused_computation.2 | convolution fusion | flops 271579136 | bytes 5054464 | tf_op jit(solution)/shard_map/cond/branch_1_fun/tgrd,sgd->tgrs/dot_general | solution.py:15
  39.7 1.9 %copy-done = f32[2,512,128,8]{2,1,3,0:T(8,128)} copy-done((f32[2,512,128,8]{2,1,3,0:T(8,128)}, f32[2,512,128,8]{2,1,3,0:T(8,128)S(1)}, u32[]{:S(2)}) %copy-start) | copy-done | bytes 4194328 | tf_op jit(solution)/shard_map/cond
  41.7 1.0 %fusion.2 = f32[128,2,8]{0,2,1:T(8,128)S(1)} fusion(f32[2,512,128,8]{2,1,3,0:T(8,128)S(1)} %get-tuple-element.43, f32[128,2,8]{0,2,1:T(8,128)S(1)} %broadcast_maximum_fusion, pred[128,512]{0,1:T(8,128)(4,1)S(1)} %broadcast_compare_fusion), kind=kLoop, calls=%fused_computation.4 | loop fusion | flops 5240832 | bytes 4276224 | tf_op jit(solution)/shard_map/cond/branch_1_fun/reduce_sum | solution.py:23
  42.8 3.7 %fusion.9 = f32[128,2,8,128]{3,0,2,1:T(8,128)S(1)} fusion(f32[2,512,128,8]{2,1,3,0:T(8,128)} %copy-done, f32[128,2,8]{0,2,1:T(8,128)S(1)} %broadcast_maximum_fusion, pred[128,512]{0,1:T(8,128)(4,1)S(1)} %broadcast_compare_fusion, f32[128,2,8]{0,2,1:T(8,128)S(1)} %get-tuple-element.40, bf16[512,2,128,1]{2,1,0,3:T(2,128)(2,1)S(1)} %bitcast.53), kind=kOutput, calls=%fused_computation.8 | convolution fusion | flops 273940480 | bytes 5586944 | tf_op jit(solution)/shard_map/cond/branch_1_fun/tgrs,sgd->tgrd/dot_general | solution.py:24
  46.5 0.3 copy.43
  46.8 0.1 divide_convert_fusion
  46.9 1.0 %copy.34 = bf16[1,128,2048]{2,1,0:T(8,128)(2,1)} copy(bf16[1,128,2048]{1,2,0:T(8,128)(2,1)S(1)} %bitcast.48) | data formatting | bytes 1048576
  47.9 0.2 fusion.26
  48.1 5.4 %psum.7 = f32[1,128]{1,0:T(1,128)} all-reduce(f32[1,128]{1,0:T(1,128)S(1)} %fusion.26), channel_id=1, replica_groups=mesh['dp'=4,'ctx'=4,'tp'=2] {'tp'}, use_global_device_ids=true, to_apply=%region_8.9 | all-reduce | flops 128 | bytes 1024 | tf_op jit(solution)/shard_map/psum | solution.py:111
  (11 shorter events, 0.3 us)
Async XLA Ops:
  4.2 11.8 %all-to-all-start = ((s32[4,4,1]{1,2,0:T(1,128)}), s32[4,4,1]{1,2,0:T(1,128)S(1)}, u32[]{:S(2)}, u32[]{:S(2)}) async-start(s32[4,4,1]{1,2,0:T(1,128)} %bitcast.7), calls=%async_computation | async-start | bytes 4096 | tf_op jit(solution)/shard_map/all_to_all | solution.py:64
  16.0 8.8 %all-to-all-start.1 = ((bf16[16,2,256]{2,1,0:T(2,128)(2,1)}), bf16[16,2,256]{2,1,0:T(2,128)(2,1)S(1)}, u32[]{:S(2)}, u32[]{:S(2)}) async-start(bf16[16,2,256]{2,1,0:T(2,128)(2,1)} %reshape.108), calls=%async_computation.1 | async-start | bytes 32768 | tf_op jit(solution)/shard_map/all_to_all | solution.py:63
  39.7 1.9 %copy-start = (f32[2,512,128,8]{2,1,3,0:T(8,128)}, f32[2,512,128,8]{2,1,3,0:T(8,128)S(1)}, u32[]{:S(2)}) copy-start(f32[2,512,128,8]{2,1,3,0:T(8,128)S(1)} %get-tuple-element.43) | copy-start | bytes 12582916 | tf_op jit(solution)/shard_map/cond
where the time goes:
time: 54.1 us; the launch traced here: 53.5 us
  blocking collectives  17 us (31%)
  starting transfers between devices  9.6 us (18%)
  local copies, waits for them, and re-layouts  7.91 us (15%)
  waiting for transfers between devices  7.34 us (14%)
  other arithmetic  5.85 us (11%)
  matrix products  5.05 us (9%)
  between operations  0.68 us (1%)
    all_to_all x1, starting transfers between devices, body(): lax.all_to_all(slot_place, 'dp', split_axis=0, concat_axis=0, tiled=True)  6.35 us
    all_gather x1, blocking collectives, body(): piece_values = lax.all_gather(merged_values, 'ctx', axis=0, tiled=True)  5.84 us
    all_gather x1, blocking collectives, body(): piece_keys = lax.all_gather(merged_keys, 'ctx', axis=0, tiled=True)  5.78 us
    psum x1, blocking collectives, body(): value_out = lax.psum(partial_value, 'tp')  5.42 us
    all_to_all x1, waiting for transfers between devices, body(): lax.all_to_all(slot_place, 'dp', split_axis=0, concat_axis=0, tiled=True)  3.85 us
    dot_general x1, matrix products, attend_block(): jnp.einsum('tgrs,sgd->tgrd', weights.astype(jnp.bfloat16), block_values,...  3.67 us
    all_to_all x1, waiting for transfers between devices, body(): lax.all_to_all(packed, 'dp', split_axis=0, concat_axis=0, tiled=True)  3.49 us
    all_to_all x1, starting transfers between devices, body(): lax.all_to_all(packed, 'dp', split_axis=0, concat_axis=0, tiled=True)  3.25 us
  transfers between devices with their start and end apart: 2, of which 2 were waited for; matrix products, arithmetic and copies ran while one was open for 7% of the time, Pallas kernels for 0%

commit v1 on v0

--- a/solution.py
+++ b/solution.py
@@ -5,6 +5,21 @@
 
 HD = 128
 CAP = 4
+
+
+def switch_the_indices(s0):
+    n_shards = jax.lax.axis_size("ctx")
+    clean = range(n_shards)
+    mid_arr = map(lambda c: (c, (c + 1) % n_shards), clean)
+    all_blocks = list(mid_arr)
+
+    def lead_sources_all_on(y2):
+        if len(y2) == n_shards:
+            return y2
+        return lead_sources_all_on([jax.lax.ppermute(y2[0], "ctx", all_blocks), *y2])
+
+    step_out = jnp.concatenate(lead_sources_all_on([s0]), axis=0)
+    return jnp.roll(step_out, (jax.lax.axis_index("ctx") + 1) * s0.shape[0], axis=0)
 
 
 def attend_block(
@@ -83,7 +98,7 @@
     )
     carried = initial
     start_row = jnp.int32(0)
-    piece_keys = lax.all_gather(merged_keys, "ctx", axis=0, tiled=True)
+    piece_keys = switch_the_indices(merged_keys)
     piece_values = lax.all_gather(merged_values, "ctx", axis=0, tiled=True)
     piece_rows = piece_keys.shape[0]
     block_rows = min(512, piece_rows)

time: 54.1 us -> 56.6 us (1.046)
  waiting for transfers between devices: 7.34 us -> 14.8 us
  blocking collectives: 17 us -> 11.6 us
    ppermute x0 -> x3, waiting for transfers between devices: none -> 6.67 us  [lead_sources_all_on(): jax.lax.ppermute(y2[0], 'ctx', all_blocks)]
    all_gather x1 -> x0, blocking collectives: 5.78 us -> none  [body(): piece_keys = lax.all_gather(merged_keys, 'ctx', axis=0, tiled=True)]
    all_to_all x1, waiting for transfers between devices: 3.49 us -> 4.32 us  [body(): lax.all_to_all(packed, 'dp', split_axis=0, concat_axis=0, tiled=True)]
    unnamed x4 -> x11, local copies, waits for them, and re-layouts: 2.41 us -> 2.46 us
  transfers between devices with their start and end apart: 2 -> 5, of which waited for: 2 -> 4; matrix products, arithmetic and copies ran while one was open for 7% -> 6% of each run, Pallas kernels for 0% -> 0%
where the time goes in v1:
time: 56.6 us; the launch traced here: 56.1 us
  waiting for transfers between devices  14.8 us (26%)
  blocking collectives  11.6 us (20%)
  starting transfers between devices  9.66 us (17%)
  local copies, waits for them, and re-layouts  8.18 us (14%)
  other arithmetic  5.81 us (10%)
  matrix products  5.14 us (9%)
  between operations  0.76 us (1%)
    ppermute x3, waiting for transfers between devices, lead_sources_all_on(): jax.lax.ppermute(y2[0], 'ctx', all_blocks)  6.67 us
    all_to_all x1, starting transfers between devices, body(): lax.all_to_all(slot_place, 'dp', split_axis=0, concat_axis=0, tiled=True)  6.35 us
    all_gather x1, blocking collectives, body(): piece_values = lax.all_gather(merged_values, 'ctx', axis=0, tiled=True)  6.21 us
    psum x1, blocking collectives, body(): value_out = lax.psum(partial_value, 'tp')  5.42 us
    all_to_all x1, waiting for transfers between devices, body(): lax.all_to_all(packed, 'dp', split_axis=0, concat_axis=0, tiled=True)  4.32 us
    all_to_all x1, waiting for transfers between devices, body(): lax.all_to_all(slot_place, 'dp', split_axis=0, concat_axis=0, tiled=True)  3.85 us
    dot_general x1, matrix products, attend_block(): jnp.einsum('tgrs,sgd->tgrd', weights.astype(jnp.bfloat16), block_values,...  3.67 us
    all_to_all x1, starting transfers between devices, body(): lax.all_to_all(packed, 'dp', split_axis=0, concat_axis=0, tiled=True)  3.25 us
  transfers between devices with their start and end apart: 5, of which 4 were waited for; matrix products, arithmetic and copies ran while one was open for 6% of the time, Pallas kernels for 0%

profile of v1, /device:TPU:0, one launch (start us, length us, event | category | flops | bytes accessed | tf_op | source)
XLA Modules:
  0.0 56.1 jit_solution(10868257774627822605)
XLA Ops:
  0.6 0.7 %fusion.24 = s32[8,4]{0,1:T(4,128)S(1)} fusion(s32[8]{0:T(128)} %bitcast.63), kind=kLoop, calls=%fused_computation.45 | loop fusion | flops 64 | bytes 160 | tf_op jit(solution)/shard_map/convert_element_type | solution.py:63
  1.3 0.2 reduce_window_sum.11
  1.5 0.7 %select_reduce_fusion.1 = s32[8]{0:T(128)S(1)} fusion(s32[8,4]{0,1:T(4,128)S(1)} %reduce_window_sum.11, s32[8]{0:T(128)} %bitcast.64), kind=kLoop, calls=%fused_computation.43 | loop fusion | flops 152 | bytes 192 | tf_op jit(solution)/shard_map/reduce_sum | solution.py:67
  2.2 0.7 %multiply_add_fusion.1 = s32[8]{0:T(128)S(1)} fusion(s32[8]{0:T(128)S(1)} %select_reduce_fusion.1, s32[1,1,8,1]{2,3,1,0:T(1,128)} %param.13), kind=kLoop, calls=%fused_computation.47 | loop fusion | flops 16 | bytes 96 | tf_op jit(solution)/shard_map/add | solution.py:68
  2.8 0.7 %convert_reduce_fusion = (s32[16]{0:T(128)S(1)}, s32[16]{0:T(128)S(1)}) fusion(s32[8]{0:T(128)S(1)} %multiply_add_fusion.1, s32[8]{0:T(128)} %bitcast.65), kind=kLoop, calls=%fused_computation.39 | loop fusion | flops 608 | bytes 192 | tf_op jit(solution)/shard_map/reduce_sum | solution.py:74
  3.6 0.7 %add.77 = s32[4,4,1]{1,0,2:T(4,128)} reshape(s32[16]{0:T(128)S(1)} %multiply_add_fusion) | data formatting | bytes 128 | tf_op jit(solution)/shard_map/add | solution.py:75
  4.2 6.3 %all-to-all-start = ((s32[4,4,1]{1,2,0:T(1,128)}), s32[4,4,1]{1,2,0:T(1,128)S(1)}, u32[]{:S(2)}, u32[]{:S(2)}) async-start(s32[4,4,1]{1,2,0:T(1,128)} %bitcast.3), calls=%async_computation | async-start | bytes 4096 | tf_op jit(solution)/shard_map/all_to_all | solution.py:79
  10.6 0.7 %copy.48 = bf16[1,8,2,256]{3,1,2,0:T(8,128)(2,1)S(1)} copy(bf16[1,8,2,256]{3,2,1,0:T(2,128)(2,1)} %bitcast.61) | data formatting | bytes 16384
  11.3 0.3 convolution_convert_fusion
  11.5 0.6 %reshape.115 = bf16[16,2,256]{2,1,0:T(2,128)(2,1)} reshape(bf16[16,512]{1,0:T(8,128)(2,1)S(1)} %convolution_convert_fusion) | data formatting | bytes 32768 | tf_op jit(solution)/shard_map/reshape | solution.py:76
  12.2 3.8 %all-to-all-done = s32[4,4,1]{1,2,0:T(1,128)S(1)} async-done(((s32[4,4,1]{1,2,0:T(1,128)}), s32[4,4,1]{1,2,0:T(1,128)S(1)}, u32[]{:S(2)}, u32[]{:S(2)}) %all-to-all-start) | async-done | bytes 96 | tf_op jit(solution)/shard_map/all_to_all | solution.py:79
  16.0 3.3 %all-to-all-start.1 = ((bf16[16,2,256]{2,1,0:T(2,128)(2,1)}), bf16[16,2,256]{2,1,0:T(2,128)(2,1)S(1)}, u32[]{:S(2)}, u32[]{:S(2)}) async-start(bf16[16,2,256]{2,1,0:T(2,128)(2,1)} %reshape.115), calls=%async_computation.1 | async-start | bytes 32768 | tf_op jit(solution)/shard_map/all_to_all | solution.py:78
  19.3 0.5 broadcast.106
  19.8 0.7 %reduce.3 = s32[4,4]{1,0:T(4,128)S(1)} reduce(s32[4,4,1]{1,2,0:T(1,128)S(1)} %all-to-all-done, s32[]{:T(128)} %broadcast.106), dimensions={2}, to_apply=%all_to_all.7.reduce_sub_computation.3 | reduce | bytes 132 | tf_op jit(solution)/shard_map/all_to_all | solution.py:79
  20.5 4.3 %all-to-all-done.1 = bf16[16,2,256]{2,1,0:T(2,128)(2,1)S(1)} async-done(((bf16[16,2,256]{2,1,0:T(2,128)(2,1)}), bf16[16,2,256]{2,1,0:T(2,128)(2,1)S(1)}, u32[]{:S(2)}, u32[]{:S(2)}) %all-to-all-start.1) | async-done | bytes 16416 | tf_op jit(solution)/shard_map/all_to_all | solution.py:78
  25.0 0.9 %fusion.19 = (bf16[128,256]{1,0:T(8,128)(2,1)S(1)}, bf16[128,256]{1,0:T(8,128)(2,1)S(1)}) fusion(f32[128,512]{1,0:T(8,128)S(1)} %fusion.21, bf16[1,128,256]{2,1,0:T(8,128)(2,1)} %param.11, bf16[1,128,256]{2,1,0:T(8,128)(2,1)} %param.10), kind=kLoop, calls=%fused_computation.24 | loop fusion | flops 196608 | bytes 524288 | tf_op jit(solution)/shard_map/convert_element_type | solution.py:88
  26.0 3.7 %collective-permute-done = bf16[128,256]{1,0:T(8,128)(2,1)S(1)} collective-permute-done((bf16[128,256]{1,0:T(8,128)(2,1)S(1)}, bf16[128,256]{1,0:T(8,128)(2,1)S(1)}, u32[]{:S(2)}, u32[]{:S(2)}) %collective-permute-start) | collective-permute-done | bytes 65568 | tf_op jit(solution)/shard_map/ppermute | solution.py:19
  29.7 0.7 %reshape.123 = bf16[2048,1]{0,1:T(2,128)(2,1)S(1)} reshape(bf16[2048]{0:T(1024)(128)(2,1)} %param.15) | data formatting | bytes 8192 | tf_op args[6]
  30.4 3.0 %collective-permute-done.1 = bf16[128,256]{1,0:T(8,128)(2,1)S(1)} collective-permute-done((bf16[128,256]{1,0:T(8,128)(2,1)S(1)}, bf16[128,256]{1,0:T(8,128)(2,1)S(1)}, u32[]{:S(2)}, u32[]{:S(2)}) %collective-permute-start.1) | collective-permute-done | bytes 65568 | tf_op jit(solution)/shard_map/ppermute | solution.py:19
  33.4 6.2 %all_gather.3 = bf16[512,256]{1,0:T(8,128)(2,1)S(1)} all-gather(bf16[128,256]{1,0:T(8,128)(2,1)S(1)} %get-tuple-element.201), channel_id=1, replica_groups=mesh['dp'=4,'ctx'=4,'tp'=2] {'ctx'}, dimensions={0}, use_global_device_ids=true | all-gather | bytes 327680 | tf_op jit(solution)/shard_map/all_gather | solution.py:102
  39.7 9.7 %conditional.1 = (f32[128,2,8]{0,2,1:T(8,128)S(1)}, f32[128,2,8,128]{0,3,2,1:T(8,128)S(1)}) conditional(s32[]{:T(128)} %convert_element_type.56, () %tuple.27, (s32[512]{0:T(512)S(1)}, s32[]{:T(128)}, s32[128]{0:T(128)S(1)}, s32[]{:T(128)}, s32[]{:T(128)}, /*index=5*/bf16[1024,256]{1,0:T(8,128)(2,1)S(1)}, bf16[1,128,2048]{2,1,0:T(8,128)(2,1)}, ...), branch_computations={%region_4.5_spmd, %region_5.8_spmd.clone} | conditional | flops 550836352 | bytes 37056208 | solution.py:116
  39.9 0.2 copy.35
  40.1 0.2 constant_dynamic-slice_fusion
  40.3 1.1 %copy.47 = bf16[16,8,16,128]{3,2,1,0:T(8,128)(2,1)S(1)} copy(bf16[16,8,16,128]{3,1,2,0:T(8,128)(2,1)} %bitcast.57) | data formatting | bytes 1048576 | tf_op jit(solution)/shard_map/cond
  41.4 0.9 %fusion = (f32[128,2,8]{0,2,1:T(8,128)S(1)}, f32[2,512,128,8]{2,1,3,0:T(8,128)S(1)}) fusion(pred[128,512]{0,1:T(8,128)(4,1)S(1)} %broadcast_compare_fusion, bf16[512,2,128,1]{0,2,3,1:T(8,128)(2,1)S(1)} %bitcast.56, bf16[128,2,8,128]{3,2,1,0:T(8,128)(2,1)S(1)} %bitcast.55), kind=kOutput, calls=%fused_computation.2 | convolution fusion | flops 271579136 | bytes 5054464 | tf_op jit(solution)/shard_map/cond/branch_1_fun/tgrd,sgd->tgrs/dot_general | solution.py:30
  42.3 1.9 %copy-done = f32[2,512,128,8]{2,1,3,0:T(8,128)} copy-done((f32[2,512,128,8]{2,1,3,0:T(8,128)}, f32[2,512,128,8]{2,1,3,0:T(8,128)S(1)}, u32[]{:S(2)}) %copy-start) | copy-done | bytes 4194328 | tf_op jit(solution)/shard_map/cond
  44.2 1.0 %fusion.2 = f32[128,2,8]{0,2,1:T(8,128)S(1)} fusion(f32[2,512,128,8]{2,1,3,0:T(8,128)S(1)} %get-tuple-element.200, f32[128,2,8]{0,2,1:T(8,128)S(1)} %broadcast_maximum_fusion, pred[128,512]{0,1:T(8,128)(4,1)S(1)} %broadcast_compare_fusion), kind=kLoop, calls=%fused_computation.4 | loop fusion | flops 5240832 | bytes 4276224 | tf_op jit(solution)/shard_map/cond/branch_1_fun/reduce_sum | solution.py:38
  45.4 3.7 %fusion.9 = f32[128,2,8,128]{3,0,2,1:T(8,128)S(1)} fusion(f32[2,512,128,8]{2,1,3,0:T(8,128)} %copy-done, f32[128,2,8]{0,2,1:T(8,128)S(1)} %broadcast_maximum_fusion, pred[128,512]{0,1:T(8,128)(4,1)S(1)} %broadcast_compare_fusion, f32[128,2,8]{0,2,1:T(8,128)S(1)} %get-tuple-element.197, bf16[512,2,128,1]{2,1,0,3:T(2,128)(2,1)S(1)} %bitcast.58), kind=kOutput, calls=%fused_computation.8 | convolution fusion | flops 273940480 | bytes 5586944 | tf_op jit(solution)/shard_map/cond/branch_1_fun/tgrs,sgd->tgrd/dot_general | solution.py:39
  49.0 0.3 copy.46
  49.5 1.0 %copy.37 = bf16[1,128,2048]{2,1,0:T(8,128)(2,1)} copy(bf16[1,128,2048]{1,2,0:T(8,128)(2,1)S(1)} %bitcast.53) | data formatting | bytes 1048576
  50.5 0.2 fusion.25
  50.7 5.4 %psum.7 = f32[1,128]{1,0:T(1,128)} all-reduce(f32[1,128]{1,0:T(1,128)S(1)} %fusion.25), channel_id=1, replica_groups=mesh['dp'=4,'ctx'=4,'tp'=2] {'tp'}, use_global_device_ids=true, to_apply=%region_8.9 | all-reduce | flops 128 | bytes 1024 | tf_op jit(solution)/shard_map/psum | solution.py:126
  (25 shorter events, 0.7 us)
Async XLA Ops:
  4.2 11.8 %all-to-all-start = ((s32[4,4,1]{1,2,0:T(1,128)}), s32[4,4,1]{1,2,0:T(1,128)S(1)}, u32[]{:S(2)}, u32[]{:S(2)}) async-start(s32[4,4,1]{1,2,0:T(1,128)} %bitcast.3), calls=%async_computation | async-start | bytes 4096 | tf_op jit(solution)/shard_map/all_to_all | solution.py:79
  16.0 8.8 %all-to-all-start.1 = ((bf16[16,2,256]{2,1,0:T(2,128)(2,1)}), bf16[16,2,256]{2,1,0:T(2,128)(2,1)S(1)}, u32[]{:S(2)}, u32[]{:S(2)}) async-start(bf16[16,2,256]{2,1,0:T(2,128)(2,1)} %reshape.115), calls=%async_computation.1 | async-start | bytes 32768 | tf_op jit(solution)/shard_map/all_to_all | solution.py:78
  25.9 3.7 %collective-permute-start = (bf16[128,256]{1,0:T(8,128)(2,1)S(1)}, bf16[128,256]{1,0:T(8,128)(2,1)S(1)}, u32[]{:S(2)}, u32[]{:S(2)}) collective-permute-start(bf16[128,256]{1,0:T(8,128)(2,1)S(1)} %get-tuple-element.202), channel_id=1, source_target_pairs={{0,2},{2,4},{4,6},{6,0},{1,3},{3,5},{5,7},{7,1},{8,10},{10,12},{12... | collective-permute-start | bytes 196616 | tf_op jit(solution)/shard_map/ppermute | solution.py:19
  29.7 3.7 %collective-permute-start.1 = (bf16[128,256]{1,0:T(8,128)(2,1)S(1)}, bf16[128,256]{1,0:T(8,128)(2,1)S(1)}, u32[]{:S(2)}, u32[]{:S(2)}) collective-permute-start(bf16[128,256]{1,0:T(8,128)(2,1)S(1)} %collective-permute-done), channel_id=1, source_target_pairs={{0,2},{2,4},{4,6},{6,0},{1,3},{3,5},{5,7},{7,1},{8,10},{10,12},{12... | collective-permute-start | bytes 196616 | tf_op jit(solution)/shard_map/ppermute | solution.py:19
  33.4 6.2 %collective-permute-start.2 = (bf16[128,256]{1,0:T(8,128)(2,1)S(1)}, bf16[128,256]{1,0:T(8,128)(2,1)S(1)}, u32[]{:S(2)}, u32[]{:S(2)}) collective-permute-start(bf16[128,256]{1,0:T(8,128)(2,1)S(1)} %collective-permute-done.1), channel_id=1, source_target_pairs={{0,2},{2,4},{4,6},{6,0},{1,3},{3,5},{5,7},{7,1},{8,10},{10,12},{12... | collective-permute-start | bytes 196616 | tf_op jit(solution)/shard_map/ppermute | solution.py:19
  42.3 1.9 %copy-start = (f32[2,512,128,8]{2,1,3,0:T(8,128)}, f32[2,512,128,8]{2,1,3,0:T(8,128)S(1)}, u32[]{:S(2)}) copy-start(f32[2,512,128,8]{2,1,3,0:T(8,128)S(1)} %get-tuple-element.200) | copy-start | bytes 12582916 | tf_op jit(solution)/shard_map/cond
